TPU v7x, 32 devices: a whole 2x2x4 slice. The times are simulated.
32 devices in a mesh: ia: 4 (over y, x), ja: 4 (over z), col: 2 (over core).
Axes of the slice: x: 2, y: 2, z: 4, core: 2. Of those that a mesh axis runs over, the one named last changes fastest.
Arguments:
- pair_rep: bfloat16 [512, 512, 128], P('ia', 'ja'), may hold values from -6 to 6
- norm_gain: float32 [128], replicated, may hold values from 0.1 to 1.9
- weights: bfloat16 [4, 128, 128], P(None, None, 'col'), may hold values from -0.5 to 0.5
- residue_mask: int32 [512], replicated, may hold values 0 or 1
- product_grad: bfloat16 [512, 128, 512], P('ia', 'col', 'ja'), may hold values from -1 to 1
Outputs:
- pair_grad: bfloat16 [512, 512, 128], P('ia', 'ja')
- weight_grads: float32 [4, 128, 128], P(None, None, 'col')
All inputs are finite; a program needn't handle non-finite values.
Results may differ from a plain program's by a relative error of at most 0.0067.
Values may be sent and summed in bfloat16 or wider, within the bound.
A program may use at most 128 MiB of HBM per device.

v0:
```python
import jax
import jax.numpy as jnp
from jax import lax
from jax.sharding import PartitionSpec as P

CLIP_LIMIT = 64.0


def gate_terms(incoming, linear, gate_pre, pair_valid):
    sigmoid_gate = jax.nn.sigmoid(gate_pre)
    through = incoming * pair_valid
    return (through * sigmoid_gate, through * linear * sigmoid_gate * (1.0 - sigmoid_gate))


def on_device(pair_rep, norm_gain, weights, residue_mask, product_grad):
    row_count = pair_rep.shape[0]
    col_count = pair_rep.shape[1]
    row_first = lax.axis_index("ia") * row_count
    col_first = lax.axis_index("ja") * col_count
    validity = residue_mask.astype(jnp.float32)
    row_valid = lax.dynamic_slice_in_dim(validity, row_first, row_count)
    col_valid = lax.dynamic_slice_in_dim(validity, col_first, col_count)
    pair_valid = row_valid[:, None, None] * col_valid[None, None, :]
    floats = pair_rep.astype(jnp.float32)
    centred = floats - jnp.mean(floats, axis=-1, keepdims=True)
    inv_std = lax.rsqrt(jnp.mean(centred * centred, axis=-1, keepdims=True) + 1e-05)
    unit_rows = centred * inv_std
    normed = (unit_rows * norm_gain).astype(jnp.bfloat16)
    projected = jnp.einsum("ikd,wdc->wick", normed, weights, preferred_element_type=jnp.float32)
    left_side = (pair_valid * jax.nn.sigmoid(projected[1]) * projected[0]).astype(jnp.bfloat16)
    right_side = (pair_valid * jax.nn.sigmoid(projected[3]) * projected[2]).astype(jnp.bfloat16)
    row_panel = lax.all_gather(product_grad, "ja", axis=2, tiled=True)
    panel_part = row_panel
    grad_left = jnp.einsum(
        "icj,jck->ick",
        panel_part,
        lax.all_gather(right_side, "ia", axis=0, tiled=True),
        preferred_element_type=jnp.float32,
    )
    panel_part = row_panel
    grad_right = lax.psum_scatter(
        jnp.einsum("icj,ick->jck", panel_part, left_side, preferred_element_type=jnp.float32),
        "ia",
        scatter_dimension=0,
        tiled=True,
    )
    lin_a, gate_a = gate_terms(grad_left, projected[0], projected[1], pair_valid)
    lin_b, gate_b = gate_terms(grad_right, projected[2], projected[3], pair_valid)
    proj_grads = jnp.stack([lin_a, gate_a, lin_b, gate_b]).astype(jnp.bfloat16)
    grad_part = jnp.einsum("ikd,wick->wdc", normed, proj_grads, preferred_element_type=jnp.float32)
    input_part = jnp.einsum(
        "wick,wdc->ikd", proj_grads, weights, preferred_element_type=jnp.float32
    )
    normed_grad = lax.psum(input_part, "col")
    scaled = normed_grad * norm_gain
    pair_grad = inv_std * (
        scaled
        - jnp.mean(scaled, axis=-1, keepdims=True)
        - unit_rows * jnp.mean(scaled * unit_rows, axis=-1, keepdims=True)
    )
    summed = lax.psum(grad_part, ("ia", "ja"))
    squares = lax.psum(jnp.sum(summed * summed), "col")
    factor = jnp.minimum(1.0, CLIP_LIMIT * lax.rsqrt(squares + 1e-06))
    weight_grads = summed * factor
    return (pair_grad.astype(jnp.bfloat16), weight_grads)


def solution(mesh):
    placed = (P("ia", "ja", None), P(), P(None, None, "col"), P(), P("ia", "col", "ja"))
    return jax.shard_map(
        on_device,
        mesh=mesh,
        in_specs=placed,
        out_specs=(P("ia", "ja", None), P(None, None, "col")),
        check_vma=False,
    )
```

profile of v0, /device:TPU:0, one launch (start us, length us, event | category | flops | bytes accessed | tf_op | source)
XLA Modules:
  0.0 660.3 jit_solution(14896707460684824877)
XLA Ops:
  7.2 4.3 copy.18
  11.8 3.5 convert_reduce_fusion
  15.3 4.8 fusion.10
  20.2 4.7 convolution_bitcast_fusion
  24.9 5.9 copy-done.1
  30.8 2.6 multiply_convert_fusion.5
  33.9 129.6 %all-gather.5.cloned.1.call-done = bf16[128,64,512]{2,0,1:T(8,128)(2,1)} async-done(((bf16[128,64,128]{2,0,1:T(8,128)(2,1)}), bf16[128,64,512]{2,0,1:T(8,128)(2,1)}) %all-gather.5.cloned.1.call-update) | async-done | bytes 8388624 | tf_op jit(solution)/shard_map/all_gather | solution.py:32
  163.5 87.5 %all-gather.3.cloned.1.call-done = bf16[512,64,128]{2,1,0:T(8,128)(2,1)} async-done(((bf16[128,64,128]{2,1,0:T(8,128)(2,1)}), bf16[512,64,128]{2,1,0:T(8,128)(2,1)}) %all-gather.3.cloned.1.call-update) | async-done | bytes 8388624 | tf_op jit(solution)/shard_map/all_gather | solution.py:37
  251.0 25.2 %fusion.11 = f32[64,128,128]{2,1,0:T(8,128)} fusion(bf16[128,64,512]{2,0,1:T(8,128)(2,1)} %all-gather.5.cloned.1.call-done, bf16[512,64,128]{2,1,0:T(8,128)(2,1)} %all-gather.3.cloned.1.call-done), kind=kOutput, calls=%fused_computation.15 | convolution fusion | flops 1073741824 | bytes 20971520 | tf_op jit(solution)/shard_map/icj,jck->ick/dot_general | solution.py:34
  276.2 5.4 copy.20
  281.6 6.8 %fusion.28 = (bf16[1,128,64,128]{3,2,1,0:T(8,128)(2,1)S(1)}, bf16[1,128,64,128]{3,2,1,0:T(8,128)(2,1)}, bf16[128,64,128]{2,1,0:T(8,128)(2,1)S(1)}) fusion(f32[64,128,128]{1,0,2:T(8,128)} %copy.20, f32[128,128]{1,0:T(8,128)S(1)} %broadcast_multiply_fusion.1, f32[4,128,64,128]{3,2,0,1:T(8,128)} %copy-done.1), kind=kLoop, calls=%fused_computation.43 | loop fusion | flops 14680064 | bytes 18939904 | tf_op jit(solution)/shard_map/stack | solution.py:49
  288.5 14.1 %fusion.32 = f32[64,128,512]{2,1,0:T(8,128)} fusion(bf16[128,64,512]{2,0,1:T(8,128)(2,1)} %all-gather.5.cloned.1.call-done, bf16[128,64,128]{2,1,0:T(8,128)(2,1)S(1)} %get-tuple-element.8), kind=kOutput, calls=%fused_computation.47 | convolution fusion | flops 1073741824 | bytes 27262976 | tf_op jit(solution)/shard_map/icj,ick->jck/dot_general | solution.py:42
  302.6 16.6 %copy.23 = f32[64,128,512]{1,0,2:T(8,128)} copy(f32[64,128,512]{2,1,0:T(8,128)} %fusion.32) | data formatting | bytes 33554432 | tf_op jit(solution)/shard_map/icj,ick->jck/dot_general | solution.py:42
  319.2 153.8 %reduce-scatter.2.cloned.1.call-done = f32[128,64,128]{2,1,0:T(8,128)} async-done(((f32[512,64,128]{2,1,0:T(8,128)}), f32[128,64,128]{2,1,0:T(8,128)}) %reduce-scatter.2.cloned.1.call-update) | async-done | bytes 4194320 | tf_op jit(solution)/shard_map/reduce_scatter | solution.py:41
  473.1 6.0 fusion.30
  481.1 5.4 fusion.34
  486.6 6.5 convolution_bitcast_fusion.1
  493.1 99.0 %all-reduce.5.cloned.1.call-done = f32[4,128,64]{1,2,0:T(8,128)} async-done(((f32[4,128,64]{1,2,0:T(8,128)}), f32[4,128,64]{1,2,0:T(8,128)}) %all-reduce.5.cloned.1.call-update) | async-done | bytes 131088 | tf_op jit(solution)/shard_map/psum | solution.py:61
  592.1 1.5 multiply_reduce_fusion.1
  593.7 3.1 psum.23
  597.4 1.6 broadcast_multiply_fusion
  599.0 32.2 %all-reduce.3.cloned.1.call-done = f32[128,128,128]{2,1,0:T(8,128)} async-done(((f32[128,128,128]{2,1,0:T(8,128)}), f32[128,128,128]{2,1,0:T(8,128)}) %all-reduce.3.cloned.1.call-update) | async-done | bytes 8388624 | tf_op jit(solution)/shard_map/psum | solution.py:54
  631.2 11.6 %multiply_reduce_fusion = (f32[128,128]{1,0:T(8,128)S(1)}, f32[128,128]{1,0:T(8,128)S(1)}) fusion(f32[128,128,128]{2,1,0:T(8,128)} %all-reduce.3.cloned.1.call-done, f32[128]{0:T(128)S(1)} %copy-done.9, f32[128,128]{1,0:T(8,128)S(1)} %add_rsqrt_fusion, f32[128,128]{1,0:T(8,128)S(1)} %broadcast_multiply_fusion.4, bf16[128,128,128]{2,1,0:T(8,128)(2,1)} %param.5), kind=kLoop, calls=%fused_computation.17 | loop fusion | flops 14647296 | bytes 12845568 | tf_op jit(solution)/shard_map/reduce_sum | solution.py:58
  642.8 10.7 %fusion.9 = bf16[128,128,128]{2,1,0:T(8,128)(2,1)} fusion(bf16[128,128,128]{2,1,0:T(8,128)(2,1)S(1)} %copy-done.4, f32[128,128,128]{2,1,0:T(8,128)S(1)} %copy-done.5, f32[128,128]{1,0:T(8,128)S(1)} %get-tuple-element.11, f32[128,128]{1,0:T(8,128)S(1)} %get-tuple-element.12, f32[128]{0:T(128)S(1)} %copy-done.9, f32[128,128]{1,0:T(8,128)S(1)} %add_rsqrt_fusion, ...), kind=kLoop, calls=%fused_computation.12 | loop fusion | flops 18874368 | bytes 17039872 | tf_op jit(solution)/shard_map/convert_element_type | solution.py:65
  (37 shorter events, 3.0 us)
Async XLA Ops:
  7.2 13.0 %copy-start = (bf16[4,128,64]{1,2,0:T(8,128)(2,1)S(1)}, bf16[4,128,64]{1,2,0:T(8,128)(2,1)}, u32[]{:S(2)}) copy-start(bf16[4,128,64]{1,2,0:T(8,128)(2,1)} %param.7) | copy-start | bytes 196612
  7.2 4.4 copy-start.10
  7.2 156.3 %all-gather.5.cloned.1.call-start = ((), (), s32[]{:S(2)}) async-start(), calls=%async_computation.2 | async-start | bytes 10485760 | tf_op jit(solution)/shard_map/all_gather | solution.py:32
  11.5 239.5 %all-gather.3.cloned.1.call-start = ((), (), s32[]{:S(2)}) async-start(), calls=%async_computation.1 | async-start | bytes 10485760 | tf_op jit(solution)/shard_map/all_gather | solution.py:37
  11.6 3.7 copy-start.2
  11.8 8.4 %copy-start.9 = (f32[128]{0:T(128)S(1)}, f32[128]{0:T(128)}, u32[]{:S(2)}) copy-start(f32[128]{0:T(128)} %param.6) | copy-start | bytes 1540
  24.9 5.9 copy-start.1
  33.4 439.6 %reduce-scatter.2.cloned.1.call-start = ((), (), s32[]{:S(2)}) async-start(), calls=%async_computation.3 | async-start | bytes 20971520 | tf_op jit(solution)/shard_map/reduce_scatter | solution.py:41
  319.2 272.9 %all-reduce.5.cloned.1.call-start = ((), (), s32[]{:S(2)}) async-start(), calls=%async_computation.5 | async-start | bytes 262144 | tf_op jit(solution)/shard_map/psum | solution.py:61
  473.1 8.0 %copy-start.3 = (bf16[128,128,128]{2,1,0:T(8,128)(2,1)S(1)}, bf16[128,128,128]{2,1,0:T(8,128)(2,1)}, u32[]{:S(2)}) copy-start(bf16[128,128,128]{2,1,0:T(8,128)(2,1)} %param.5) | copy-start | bytes 12582916
  473.1 8.0 %copy-start.6 = (bf16[1,128,64,128]{3,2,1,0:T(8,128)(2,1)S(1)}, bf16[1,128,64,128]{3,2,1,0:T(8,128)(2,1)}, u32[]{:S(2)}) copy-start(bf16[1,128,64,128]{3,2,1,0:T(8,128)(2,1)} %get-tuple-element.5) | copy-start | bytes 6291460
  479.1 1.3 copy-start.7
  479.1 2.0 copy-start.8
  486.6 144.6 %all-reduce.3.cloned.1.call-start = ((), (), s32[]{:S(2)}) async-start(), calls=%async_computation.4 | async-start | bytes 16777216 | tf_op jit(solution)/shard_map/psum | solution.py:54
  631.2 11.6 %copy-start.4 = (bf16[128,128,128]{2,1,0:T(8,128)(2,1)S(1)}, bf16[128,128,128]{2,1,0:T(8,128)(2,1)}, u32[]{:S(2)}) copy-start(bf16[128,128,128]{2,1,0:T(8,128)(2,1)} %param.5) | copy-start | bytes 12582916
  631.2 11.6 %copy-start.5 = (f32[128,128,128]{2,1,0:T(8,128)S(1)}, f32[128,128,128]{2,1,0:T(8,128)}, u32[]{:S(2)}) copy-start(f32[128,128,128]{2,1,0:T(8,128)} %all-reduce.3.cloned.1.call-done) | copy-start | bytes 25165828
Sparse Core Ops, SparseCore 0:
  11.6 151.8 all-gather.4
  165.4 85.6 all-gather.2
  319.3 153.7 reduce-scatter.1
  486.7 105.3 all-reduce.4
  594.4 36.6 all-reduce.2
where the time goes:
time: 668 us; the launch traced here: 660 us
  waiting for transfers between devices  502 us (75%)
  matrix products  55.9 us (8%)
  other arithmetic  49.3 us (7%)
  local copies, waits for them, and re-layouts  34.2 us (5%)
  between operations  14.9 us (2%)
    reduce_scatter x1, waiting for transfers between devices, on_device(): lax.psum_scatter(jnp.einsum('icj,ick->jck', panel_part, left_side, prefer...  154 us
    all_gather x1, waiting for transfers between devices, on_device(): row_panel = lax.all_gather(product_grad, 'ja', axis=2, tiled=True)  130 us
    psum x1, waiting for transfers between devices, on_device(): summed = lax.psum(grad_part, ('ia', 'ja'))  99 us
    all_gather x1, waiting for transfers between devices, on_device(): lax.all_gather(right_side, 'ia', axis=0, tiled=True)  87.5 us
    psum x1, waiting for transfers between devices, on_device(): normed_grad = lax.psum(input_part, 'col')  32.2 us
    dot_general x1, matrix products, on_device(): jnp.einsum('icj,jck->ick', panel_part, lax.all_gather(right_side, 'ia', a...  25.2 us
    dot_general x1, local copies, waits for them, and re-layouts, on_device(): jnp.einsum('icj,ick->jck', panel_part, left_side, preferred_element_type=...  16.6 us
    dot_general x1, matrix products, on_device(): jnp.einsum('icj,ick->jck', panel_part, left_side, preferred_element_type=...  14.1 us
  transfers between devices with their start and end apart: 5, of which 5 were waited for; matrix products, arithmetic and copies ran while one was open for 4% of the time, Pallas kernels for 0%

commit v1 on v0

--- a/solution.py
+++ b/solution.py
@@ -58,7 +58,7 @@
         - jnp.mean(scaled, axis=-1, keepdims=True)
         - unit_rows * jnp.mean(scaled * unit_rows, axis=-1, keepdims=True)
     )
-    summed = lax.psum(grad_part, ("ia", "ja"))
+    summed = lax.psum(lax.psum(grad_part, "ja"), "ia")
     squares = lax.psum(jnp.sum(summed * summed), "col")
     factor = jnp.minimum(1.0, CLIP_LIMIT * lax.rsqrt(squares + 1e-06))
     weight_grads = summed * factor

time: 668 us -> 643 us (0.963)
  waiting for transfers between devices: 502 us -> 477 us
    psum x1 -> x2, waiting for transfers between devices: 99 us -> 72.8 us  [on_device(): summed = lax.psum(lax.psum(grad_part, 'ja'), 'ia')]
  transfers between devices with their start and end apart: 5 -> 6, of which waited for: 5 -> 6; matrix products, arithmetic and copies ran while one was open for 4% -> 4% of each run, Pallas kernels for 0% -> 0%
where the time goes in v1:
time: 643 us; the launch traced here: 635 us
  waiting for transfers between devices  477 us (74%)
  matrix products  55.9 us (9%)
  other arithmetic  49.3 us (8%)
  local copies, waits for them, and re-layouts  34.2 us (5%)
  between operations  15.2 us (2%)
    reduce_scatter x1, waiting for transfers between devices, on_device(): lax.psum_scatter(jnp.einsum('icj,ick->jck', panel_part, left_side, prefer...  154 us
    all_gather x1, waiting for transfers between devices, on_device(): row_panel = lax.all_gather(product_grad, 'ja', axis=2, tiled=True)  130 us
    all_gather x1, waiting for transfers between devices, on_device(): lax.all_gather(right_side, 'ia', axis=0, tiled=True)  87.5 us
    psum x2, waiting for transfers between devices, on_device(): summed = lax.psum(lax.psum(grad_part, 'ja'), 'ia')  72.8 us
    psum x1, waiting for transfers between devices, on_device(): normed_grad = lax.psum(input_part, 'col')  33.1 us
    dot_general x1, matrix products, on_device(): jnp.einsum('icj,jck->ick', panel_part, lax.all_gather(right_side, 'ia', a...  25.2 us
    dot_general x1, local copies, waits for them, and re-layouts, on_device(): jnp.einsum('icj,ick->jck', panel_part, left_side, preferred_element_type=...  16.6 us
    dot_general x1, matrix products, on_device(): jnp.einsum('icj,ick->jck', panel_part, left_side, preferred_element_type=...  14.1 us
  transfers between devices with their start and end apart: 6, of which 6 were waited for; matrix products, arithmetic and copies ran while one was open for 4% of the time, Pallas kernels for 0%

profile of v1, /device:TPU:0, one launch (start us, length us, event | category | flops | bytes accessed | tf_op | source)
XLA Modules:
  0.0 635.5 jit_solution(1944610599505219290)
XLA Ops:
  7.2 4.3 copy.18
  11.8 3.5 convert_reduce_fusion
  15.3 4.8 fusion.10
  20.2 4.7 convolution_bitcast_fusion
  24.9 5.9 copy-done.1
  30.8 2.6 multiply_convert_fusion.5
  33.9 129.6 %all-gather.5.cloned.1.call-done = bf16[128,64,512]{2,0,1:T(8,128)(2,1)} async-done(((bf16[128,64,128]{2,0,1:T(8,128)(2,1)}), bf16[128,64,512]{2,0,1:T(8,128)(2,1)}) %all-gather.5.cloned.1.call-update) | async-done | bytes 8388624 | tf_op jit(solution)/shard_map/all_gather | solution.py:32
  163.5 87.5 %all-gather.3.cloned.1.call-done = bf16[512,64,128]{2,1,0:T(8,128)(2,1)} async-done(((bf16[128,64,128]{2,1,0:T(8,128)(2,1)}), bf16[512,64,128]{2,1,0:T(8,128)(2,1)}) %all-gather.3.cloned.1.call-update) | async-done | bytes 8388624 | tf_op jit(solution)/shard_map/all_gather | solution.py:37
  251.0 25.2 %fusion.11 = f32[64,128,128]{2,1,0:T(8,128)} fusion(bf16[128,64,512]{2,0,1:T(8,128)(2,1)} %all-gather.5.cloned.1.call-done, bf16[512,64,128]{2,1,0:T(8,128)(2,1)} %all-gather.3.cloned.1.call-done), kind=kOutput, calls=%fused_computation.15 | convolution fusion | flops 1073741824 | bytes 20971520 | tf_op jit(solution)/shard_map/icj,jck->ick/dot_general | solution.py:34
  276.2 5.4 copy.20
  281.6 6.8 %fusion.28 = (bf16[1,128,64,128]{3,2,1,0:T(8,128)(2,1)S(1)}, bf16[1,128,64,128]{3,2,1,0:T(8,128)(2,1)}, bf16[128,64,128]{2,1,0:T(8,128)(2,1)S(1)}) fusion(f32[64,128,128]{1,0,2:T(8,128)} %copy.20, f32[128,128]{1,0:T(8,128)S(1)} %broadcast_multiply_fusion.1, f32[4,128,64,128]{3,2,0,1:T(8,128)} %copy-done.1), kind=kLoop, calls=%fused_computation.43 | loop fusion | flops 14680064 | bytes 18939904 | tf_op jit(solution)/shard_map/stack | solution.py:49
  288.5 14.1 %fusion.32 = f32[64,128,512]{2,1,0:T(8,128)} fusion(bf16[128,64,512]{2,0,1:T(8,128)(2,1)} %all-gather.5.cloned.1.call-done, bf16[128,64,128]{2,1,0:T(8,128)(2,1)S(1)} %get-tuple-element.8), kind=kOutput, calls=%fused_computation.47 | convolution fusion | flops 1073741824 | bytes 27262976 | tf_op jit(solution)/shard_map/icj,ick->jck/dot_general | solution.py:42
  302.6 16.6 %copy.23 = f32[64,128,512]{1,0,2:T(8,128)} copy(f32[64,128,512]{2,1,0:T(8,128)} %fusion.32) | data formatting | bytes 33554432 | tf_op jit(solution)/shard_map/icj,ick->jck/dot_general | solution.py:42
  319.2 153.8 %reduce-scatter.2.cloned.1.call-done = f32[128,64,128]{2,1,0:T(8,128)} async-done(((f32[512,64,128]{2,1,0:T(8,128)}), f32[128,64,128]{2,1,0:T(8,128)}) %reduce-scatter.2.cloned.1.call-update) | async-done | bytes 4194320 | tf_op jit(solution)/shard_map/reduce_scatter | solution.py:41
  473.1 6.0 fusion.30
  481.1 5.4 fusion.34
  486.6 34.7 %all-reduce.6.cloned.1.call-done = f32[4,128,64]{1,2,0:T(8,128)} async-done(((f32[4,128,64]{1,2,0:T(8,128)}), f32[4,128,64]{1,2,0:T(8,128)}) %all-reduce.6.cloned.1.call-update) | async-done | bytes 131088 | tf_op jit(solution)/shard_map/psum | solution.py:61
  521.4 6.5 %convolution_bitcast_fusion.1 = f32[128,128,128]{2,1,0:T(8,128)} fusion(bf16[1,128,64,128]{3,2,1,0:T(8,128)(2,1)} %copy-done.8, bf16[1,128,64,128]{3,2,1,0:T(8,128)(2,1)} %copy-done.7, bf16[1,128,64,128]{3,2,1,0:T(8,128)(2,1)} %get-tuple-element.5, bf16[1,128,64,128]{3,2,1,0:T(8,128)(2,1)S(1)} %get-tuple-element.4, bf16[4,128,64]{1,2,0:T(8,128)(2,1)S(1)} %copy-done), kind=kOutput, calls=%fused_computation.42 | convolution fusion | flops 1086324736 | bytes 16842752 | tf_op jit(solution)/shard_map/wick,wdc->ikd/dot_general | solution.py:51
  527.9 38.1 %all-reduce.8.cloned.1.call-done = f32[4,128,64]{1,2,0:T(8,128)} async-done(((f32[4,128,64]{1,2,0:T(8,128)}), f32[4,128,64]{1,2,0:T(8,128)}) %all-reduce.8.cloned.1.call-update) | async-done | bytes 131088 | tf_op jit(solution)/shard_map/psum | solution.py:61
  567.5 3.1 psum.31
  571.3 1.6 broadcast_multiply_fusion
  572.9 33.1 %all-reduce.4.cloned.1.call-done = f32[128,128,128]{2,1,0:T(8,128)} async-done(((f32[128,128,128]{2,1,0:T(8,128)}), f32[128,128,128]{2,1,0:T(8,128)}) %all-reduce.4.cloned.1.call-update) | async-done | bytes 8388624 | tf_op jit(solution)/shard_map/psum | solution.py:54
  606.0 11.6 %multiply_reduce_fusion = (f32[128,128]{1,0:T(8,128)S(1)}, f32[128,128]{1,0:T(8,128)S(1)}) fusion(f32[128,128,128]{2,1,0:T(8,128)} %all-reduce.4.cloned.1.call-done, f32[128]{0:T(128)S(1)} %copy-done.9, f32[128,128]{1,0:T(8,128)S(1)} %add_rsqrt_fusion, f32[128,128]{1,0:T(8,128)S(1)} %broadcast_multiply_fusion.4, bf16[128,128,128]{2,1,0:T(8,128)(2,1)} %param.5), kind=kLoop, calls=%fused_computation.17 | loop fusion | flops 14647296 | bytes 12845568 | tf_op jit(solution)/shard_map/reduce_sum | solution.py:58
  617.7 10.7 %fusion.9 = bf16[128,128,128]{2,1,0:T(8,128)(2,1)} fusion(bf16[128,128,128]{2,1,0:T(8,128)(2,1)S(1)} %copy-done.4, f32[128,128,128]{2,1,0:T(8,128)S(1)} %copy-done.5, f32[128,128]{1,0:T(8,128)S(1)} %get-tuple-element.11, f32[128,128]{1,0:T(8,128)S(1)} %get-tuple-element.12, f32[128]{0:T(128)S(1)} %copy-done.9, f32[128,128]{1,0:T(8,128)S(1)} %add_rsqrt_fusion, ...), kind=kLoop, calls=%fused_computation.12 | loop fusion | flops 18874368 | bytes 17039872 | tf_op jit(solution)/shard_map/convert_element_type | solution.py:65
  (40 shorter events, 4.6 us)
Async XLA Ops:
  7.2 13.0 %copy-start = (bf16[4,128,64]{1,2,0:T(8,128)(2,1)S(1)}, bf16[4,128,64]{1,2,0:T(8,128)(2,1)}, u32[]{:S(2)}) copy-start(bf16[4,128,64]{1,2,0:T(8,128)(2,1)} %param.7) | copy-start | bytes 196612
  7.2 4.4 copy-start.10
  7.2 156.3 %all-gather.5.cloned.1.call-start = ((), (), s32[]{:S(2)}) async-start(), calls=%async_computation.2 | async-start | bytes 10485760 | tf_op jit(solution)/shard_map/all_gather | solution.py:32
  11.5 239.5 %all-gather.3.cloned.1.call-start = ((), (), s32[]{:S(2)}) async-start(), calls=%async_computation.1 | async-start | bytes 10485760 | tf_op jit(solution)/shard_map/all_gather | solution.py:37
  11.6 3.7 copy-start.2
  11.8 8.4 %copy-start.9 = (f32[128]{0:T(128)S(1)}, f32[128]{0:T(128)}, u32[]{:S(2)}) copy-start(f32[128]{0:T(128)} %param.6) | copy-start | bytes 1540
  24.9 5.9 copy-start.1
  33.4 439.6 %reduce-scatter.2.cloned.1.call-start = ((), (), s32[]{:S(2)}) async-start(), calls=%async_computation.3 | async-start | bytes 20971520 | tf_op jit(solution)/shard_map/reduce_scatter | solution.py:41
  319.2 202.1 %all-reduce.6.cloned.1.call-start = ((), (), s32[]{:S(2)}) async-start(), calls=%async_computation.5 | async-start | bytes 262144 | tf_op jit(solution)/shard_map/psum | solution.py:61
  473.1 8.0 %copy-start.3 = (bf16[128,128,128]{2,1,0:T(8,128)(2,1)S(1)}, bf16[128,128,128]{2,1,0:T(8,128)(2,1)}, u32[]{:S(2)}) copy-start(bf16[128,128,128]{2,1,0:T(8,128)(2,1)} %param.5) | copy-start | bytes 12582916
  473.1 8.0 %copy-start.6 = (bf16[1,128,64,128]{3,2,1,0:T(8,128)(2,1)S(1)}, bf16[1,128,64,128]{3,2,1,0:T(8,128)(2,1)}, u32[]{:S(2)}) copy-start(bf16[1,128,64,128]{3,2,1,0:T(8,128)(2,1)} %get-tuple-element.5) | copy-start | bytes 6291460
  479.1 1.3 copy-start.7
  479.1 2.0 copy-start.8
  486.6 79.4 %all-reduce.8.cloned.1.call-start = ((), (), s32[]{:S(2)}) async-start(), calls=%async_computation.6 | async-start | bytes 262144 | tf_op jit(solution)/shard_map/psum | solution.py:61
  521.4 84.6 %all-reduce.4.cloned.1.call-start = ((), (), s32[]{:S(2)}) async-start(), calls=%async_computation.4 | async-start | bytes 16777216 | tf_op jit(solution)/shard_map/psum | solution.py:54
  606.0 11.6 %copy-start.4 = (bf16[128,128,128]{2,1,0:T(8,128)(2,1)S(1)}, bf16[128,128,128]{2,1,0:T(8,128)(2,1)}, u32[]{:S(2)}) copy-start(bf16[128,128,128]{2,1,0:T(8,128)(2,1)} %param.5) | copy-start | bytes 12582916
  606.0 11.6 %copy-start.5 = (f32[128,128,128]{2,1,0:T(8,128)S(1)}, f32[128,128,128]{2,1,0:T(8,128)}, u32[]{:S(2)}) copy-start(f32[128,128,128]{2,1,0:T(8,128)} %all-reduce.4.cloned.1.call-done) | copy-start | bytes 25165828
Sparse Core Ops, SparseCore 0:
  11.6 151.8 all-gather.4
  165.4 85.6 all-gather.2
  319.3 153.7 reduce-scatter.1
  486.7 34.6 all-reduce.5
  524.1 41.8 all-reduce.7
  568.3 37.6 all-reduce.3
